TPU v7x, 32 devices: a whole 2x2x4 slice. The times are simulated.
32 devices in a mesh: row: 16 (over z, y, x), col: 2 (over core).
Axes of the slice: x: 2, y: 2, z: 4, core: 2. Of those that a mesh axis runs over, the one named last changes fastest.
Arguments:
- right_sides: bfloat16 [256, 128, 128], P('row'), may hold values from -6 to 6
- inverse_diag: bfloat16 [256, 128, 128], P('row'), may hold values from -0.5 to 0.5
- off_blocks: bfloat16 [2, 256, 6, 128, 128], P('col', 'row'), may hold values from -0.09375 to 0.09375
- owners: int32 [2, 256, 6], P('col', 'row'), may hold values from 0 to 15, all different within a row; in each aligned block of 16 rows (0 to 15, 16 to 31, ..., all dimensions but the last counted through in order) at most 8 rows name the same one
- local_block: int32 [2, 256, 6], P('col', 'row'), may hold values from 0 to 15
- counts: int32 [256], P('row'), may hold values from 6 to 12
Outputs:
- solved: bfloat16 [256, 128, 128], P('row')
Inputs may be any that keep to these rules, and one draw needn't show every extreme that they name: In the 16 block rows of one device (aligned blocks of rows of the [2, 256] layout) a row's 6 entries are different owners, no owner is named more than 8 times, and in some blocks one owner exactly 8 times.
All inputs are finite; a program needn't handle non-finite values.
Results may differ from a plain program's by a relative error of at most 0.014.
Values may be sent and summed in bfloat16 or wider, within the bound.
A program may use at most 64 MiB of HBM per device.

v0:
```python
import jax
import jax.numpy as jnp
from jax import lax
from jax.sharding import PartitionSpec as P

ITERS = 4


def apply_inverse(inverse, right):
    return jnp.einsum("bij,bjr->bir", inverse, right, preferred_element_type=jnp.float32).astype(
        jnp.bfloat16
    )


def shards(right_sides, inverse_diag, off_blocks, owners, local_block, counts):
    row_count = lax.axis_size("row")
    col_index = lax.axis_index("col")
    col_count = lax.axis_size("col")
    block_rows = counts.shape[0]
    per_group = owners.shape[2]
    owner_flat = owners.reshape(-1)
    local_flat = local_block.reshape(-1)
    slot_total = owner_flat.shape[0]
    capacity = max(2, 4 * slot_total // (3 * row_count))
    one_hot = (owner_flat[:, None] == jnp.arange(row_count, dtype=jnp.int32)[None, :]).astype(
        jnp.int32
    )
    earlier = jnp.cumsum(one_hot, axis=0) - one_hot
    bucket_rank = jnp.sum(earlier * one_hot, axis=1)
    slot_place = owner_flat * capacity + bucket_rank
    requests = jnp.zeros((row_count * capacity,), jnp.int32).at[slot_place].set(local_flat)
    wanted = lax.all_to_all(
        requests.reshape(row_count, capacity), "row", split_axis=0, concat_axis=0, tiled=True
    ).reshape(-1)
    global_slot = col_index + col_count * jnp.arange(per_group, dtype=jnp.int32)
    is_live = global_slot[None, :] < counts[:, None]
    masked = jnp.where(is_live[:, :, None, None], off_blocks[0], jnp.zeros((), jnp.bfloat16))
    solved = apply_inverse(inverse_diag, right_sides)
    share_rows = block_rows // col_count
    for iteration in range(ITERS - 1):
        outgoing = solved[wanted].reshape(row_count, capacity, solved.shape[1], solved.shape[2])
        received = lax.all_to_all(outgoing, "row", split_axis=0, concat_axis=0, tiled=True)
        columns_here = received.shape[3]
        flattened = received.reshape(row_count * capacity, received.shape[2], columns_here)
        picked = flattened[slot_place].reshape(
            block_rows, per_group, received.shape[2], columns_here
        )
        partial_value = jnp.einsum(
            "bkij,bkjr->bir", masked, picked, preferred_element_type=jnp.float32
        )
        own_sums = lax.psum_scatter(
            partial_value.astype(jnp.bfloat16), "col", scatter_dimension=0, tiled=True
        ).astype(jnp.float32)
        first_row = col_index * share_rows
        right_part = lax.dynamic_slice_in_dim(right_sides, first_row, share_rows, 0).astype(
            jnp.float32
        )
        inverse_part = lax.dynamic_slice_in_dim(inverse_diag, first_row, share_rows, 0)
        corrected = (right_part - own_sums).astype(jnp.bfloat16)
        solved = lax.all_gather(apply_inverse(inverse_part, corrected), "col", axis=0, tiled=True)
    return solved


def solution(mesh):
    in_specs = (
        P("row", None, None),
        P("row", None, None),
        P("col", "row", None, None, None),
        P("col", "row", None),
        P("col", "row", None),
        P("row"),
    )
    out_specs = P("row", None, None)
    return jax.shard_map(shards, mesh=mesh, in_specs=in_specs, out_specs=out_specs, check_vma=False)
```

profile of v0, /device:TPU:0, one launch (start us, length us, event | category | flops | bytes accessed | tf_op | source)
XLA Modules:
  0.0 402.8 jit_solution(15146222344782903589)
XLA Ops:
  6.5 0.0 copy-start
  6.5 0.7 broadcast_multiply_fusion
  7.3 0.8 copy.14
  8.0 0.1 copy.13
  8.1 0.1 mul.35
  8.2 0.8 copy.15
  9.0 0.1 reshape.192
  9.1 0.1 eq.15
  9.2 0.1 fusion.24
  9.3 0.1 reduce_window_sum.11
  9.4 0.2 select_reduce_fusion
  9.6 0.9 scatter_custom_fusion
  10.5 0.7 all_to_all.15
  11.2 8.3 %all-to-all-start = ((s32[16,1,8]{2,1,0:T(1,128)}), s32[16,1,8]{2,1,0:T(1,128)S(1)}, u32[]{:S(2)}, u32[]{:S(2)}) async-start(s32[16,1,8]{2,1,0:T(1,128)} %bitcast.3), calls=%async_computation | async-start | bytes 16384 | tf_op jit(solution)/shard_map/all_to_all | solution.py:32
  19.5 0.0 copy-done
  19.5 1.3 convolution_convert_fusion
  20.9 5.9 %all-to-all-done = s32[16,1,8]{2,1,0:T(1,128)S(1)} async-done(((s32[16,1,8]{2,1,0:T(1,128)}), s32[16,1,8]{2,1,0:T(1,128)S(1)}, u32[]{:S(2)}, u32[]{:S(2)}) %all-to-all-start) | async-done | bytes 544 | tf_op jit(solution)/shard_map/all_to_all | solution.py:32
  26.7 0.5 broadcast.118
  27.2 0.7 reduce.3
  27.9 0.1 reshape.130
  28.0 3.1 gather_fusion
  31.1 0.0 copy-start.2
  31.1 4.7 %all-to-all-start.1 = ((bf16[16,8,128,128]{3,2,1,0:T(8,128)(2,1)}), bf16[16,8,128,128]{3,2,1,0:T(8,128)(2,1)}, u32[]{:S(2)}, u32[]{:S(2)}) async-start(bf16[16,8,128,128]{3,2,1,0:T(8,128)(2,1)} %bitcast.56), calls=%async_computation.1 | async-start | bytes 8388608 | tf_op jit(solution)/shard_map/all_to_all | solution.py:42
  35.8 0.0 reduce-scatter.4.cloned.1.call-start
  35.8 0.0 copy-done.2
  35.8 0.1 broadcast_compare_fusion
  35.9 78.3 %all-to-all-done.1 = bf16[16,8,128,128]{3,2,1,0:T(8,128)(2,1)} async-done(((bf16[16,8,128,128]{3,2,1,0:T(8,128)(2,1)}), bf16[16,8,128,128]{3,2,1,0:T(8,128)(2,1)}, u32[]{:S(2)}, u32[]{:S(2)}) %all-to-all-start.1) | async-done | bytes 4194336 | tf_op jit(solution)/shard_map/all_to_all | solution.py:42
  114.2 4.9 %gather_fusion.1 = bf16[96,128,128]{2,1,0:T(8,128)(2,1)} fusion(bf16[128,128,128]{2,1,0:T(8,128)(2,1)} %bitcast.6, s32[1024]{0:T(1024)S(1)} %pad_clamp_fusion), kind=kCustom, calls=%fused_computation.1 | custom fusion | bytes 6291840 | tf_op jit(solution)/shard_map/gather | solution.py:45
  119.1 0.0 copy-start.1
  119.1 4.7 %fusion.11 = bf16[16,128,128]{2,1,0:T(8,128)(2,1)} fusion(bf16[16,6,128,128]{3,2,1,0:T(8,128)(2,1)} %bitcast.62, bf16[1,16,6,128,128]{4,3,2,1,0:T(8,128)(2,1)} %param.8, pred[16,6]{1,0:T(8,128)(4,1)S(1)} %broadcast_compare_fusion), kind=kOutput, calls=%fused_computation.20 | convolution fusion | flops 404488192 | bytes 6815840 | tf_op jit(solution)/shard_map/bkij,bkjr->bir/dot_general | solution.py:48
  123.9 0.0 reduce-scatter.4.cloned.1.call-update
  123.9 0.0 reduce-scatter.6.cloned.1.call-start
  123.9 21.2 %reduce-scatter.4.cloned.1.call-done = bf16[8,128,128]{2,1,0:T(8,128)(2,1)} async-done(((bf16[16,128,128]{2,1,0:T(8,128)(2,1)}), bf16[8,128,128]{2,1,0:T(8,128)(2,1)}) %reduce-scatter.4.cloned.1.call-update) | async-done | bytes 262160 | tf_op jit(solution)/shard_map/reduce_scatter | solution.py:51
  145.1 0.0 copy-done.1
  145.1 1.2 convolution_convert_fusion.3
  146.3 2.2 all_gather.9
  148.5 3.1 gather_fusion.2
  151.5 101.0 %all_to_all.24 = bf16[16,8,128,128]{3,2,1,0:T(8,128)(2,1)} all-to-all(bf16[16,8,128,128]{3,2,1,0:T(8,128)(2,1)} %bitcast.58), channel_id=1, replica_groups=mesh['row'=16,'col'=2] {'row'}, dimensions={0} | all-to-all | bytes 8388608 | tf_op jit(solution)/shard_map/all_to_all | solution.py:42
  252.5 4.9 %gather_fusion.3 = bf16[96,128,128]{2,1,0:T(8,128)(2,1)} fusion(bf16[128,128,128]{2,1,0:T(8,128)(2,1)} %bitcast.60, s32[1024]{0:T(1024)S(1)} %pad_clamp_fusion), kind=kCustom, calls=%fused_computation.3 | custom fusion | bytes 6291840 | tf_op jit(solution)/shard_map/gather | solution.py:45
  257.4 4.7 %fusion.10 = bf16[16,128,128]{2,1,0:T(8,128)(2,1)} fusion(bf16[16,6,128,128]{3,2,1,0:T(8,128)(2,1)} %bitcast.63, bf16[1,16,6,128,128]{4,3,2,1,0:T(8,128)(2,1)} %param.8, pred[16,6]{1,0:T(8,128)(4,1)S(1)} %broadcast_compare_fusion), kind=kOutput, calls=%fused_computation.19 | convolution fusion | flops 404488192 | bytes 6815840 | tf_op jit(solution)/shard_map/bkij,bkjr->bir/dot_general | solution.py:48
  262.1 0.0 reduce-scatter.6.cloned.1.call-update
  262.1 0.0 reduce-scatter.8.cloned.1.call-start
  262.2 6.5 %reduce-scatter.6.cloned.1.call-done = bf16[8,128,128]{2,1,0:T(8,128)(2,1)} async-done(((bf16[16,128,128]{2,1,0:T(8,128)(2,1)}), bf16[8,128,128]{2,1,0:T(8,128)(2,1)}) %reduce-scatter.6.cloned.1.call-update) | async-done | bytes 262160 | tf_op jit(solution)/shard_map/reduce_scatter | solution.py:51
  268.6 1.2 convolution_convert_fusion.2
  269.8 2.2 all_gather.10
  272.0 3.1 gather_fusion.4
  275.0 101.0 %all_to_all.25 = bf16[16,8,128,128]{3,2,1,0:T(8,128)(2,1)} all-to-all(bf16[16,8,128,128]{3,2,1,0:T(8,128)(2,1)} %bitcast.57), channel_id=1, replica_groups=mesh['row'=16,'col'=2] {'row'}, dimensions={0} | all-to-all | bytes 8388608 | tf_op jit(solution)/shard_map/all_to_all | solution.py:42
  376.0 4.9 %gather_fusion.5 = bf16[96,128,128]{2,1,0:T(8,128)(2,1)} fusion(bf16[128,128,128]{2,1,0:T(8,128)(2,1)} %bitcast.59, s32[1024]{0:T(1024)S(1)} %pad_clamp_fusion), kind=kCustom, calls=%fused_computation.5 | custom fusion | bytes 6291840 | tf_op jit(solution)/shard_map/gather | solution.py:45
  380.9 4.7 %fusion.9 = bf16[16,128,128]{2,1,0:T(8,128)(2,1)} fusion(bf16[16,6,128,128]{3,2,1,0:T(8,128)(2,1)} %bitcast.61, bf16[1,16,6,128,128]{4,3,2,1,0:T(8,128)(2,1)} %param.8, pred[16,6]{1,0:T(8,128)(4,1)S(1)} %broadcast_compare_fusion), kind=kOutput, calls=%fused_computation.18 | convolution fusion | flops 404488192 | bytes 6815840 | tf_op jit(solution)/shard_map/bkij,bkjr->bir/dot_general | solution.py:48
  385.6 0.0 reduce-scatter.8.cloned.1.call-update
  385.6 6.5 %reduce-scatter.8.cloned.1.call-done = bf16[8,128,128]{2,1,0:T(8,128)(2,1)} async-done(((bf16[16,128,128]{2,1,0:T(8,128)(2,1)}), bf16[8,128,128]{2,1,0:T(8,128)(2,1)}) %reduce-scatter.8.cloned.1.call-update) | async-done | bytes 262160 | tf_op jit(solution)/shard_map/reduce_scatter | solution.py:51
  392.1 1.2 convolution_convert_fusion.1
  393.3 2.2 all_gather.11
  395.5 0.8 copy.21
  (5 shorter events, 0.0 us)
Async XLA Ops:
  6.5 13.0 %copy-start = (bf16[16,128,128]{2,1,0:T(8,128)(2,1)S(1)}, bf16[16,128,128]{2,1,0:T(8,128)(2,1)}, u32[]{:S(2)}) copy-start(bf16[16,128,128]{2,1,0:T(8,128)(2,1)} %param.7) | copy-start | bytes 1572868
  11.2 15.6 %all-to-all-start = ((s32[16,1,8]{2,1,0:T(1,128)}), s32[16,1,8]{2,1,0:T(1,128)S(1)}, u32[]{:S(2)}, u32[]{:S(2)}) async-start(s32[16,1,8]{2,1,0:T(1,128)} %bitcast.3), calls=%async_computation | async-start | bytes 16384 | tf_op jit(solution)/shard_map/all_to_all | solution.py:32
  31.1 4.8 %copy-start.2 = (s32[16]{0:T(128)S(1)}, s32[16]{0:T(128)}, u32[]{:S(2)}) copy-start(s32[16]{0:T(128)} %param.11) | copy-start | bytes 196
  31.1 83.1 %all-to-all-start.1 = ((bf16[16,8,128,128]{3,2,1,0:T(8,128)(2,1)}), bf16[16,8,128,128]{3,2,1,0:T(8,128)(2,1)}, u32[]{:S(2)}, u32[]{:S(2)}) async-start(bf16[16,8,128,128]{3,2,1,0:T(8,128)(2,1)} %bitcast.56), calls=%async_computation.1 | async-start | bytes 8388608 | tf_op jit(solution)/shard_map/all_to_all | solution.py:42
  35.8 109.4 %reduce-scatter.4.cloned.1.call-start = ((), (), s32[]{:S(2)}) async-start(), calls=%async_computation.7 | async-start | bytes 786432 | tf_op jit(solution)/shard_map/reduce_scatter | solution.py:51
  119.1 26.0 %copy-start.1 = (bf16[16,128,128]{2,1,0:T(8,128)(2,1)S(1)}, bf16[16,128,128]{2,1,0:T(8,128)(2,1)}, u32[]{:S(2)}) copy-start(bf16[16,128,128]{2,1,0:T(8,128)(2,1)} %param.6) | copy-start | bytes 1572868
  123.9 144.7 %reduce-scatter.6.cloned.1.call-start = ((), (), s32[]{:S(2)}) async-start(), calls=%async_computation.8 | async-start | bytes 786432 | tf_op jit(solution)/shard_map/reduce_scatter | solution.py:51
  262.1 130.0 %reduce-scatter.8.cloned.1.call-start = ((), (), s32[]{:S(2)}) async-start(), calls=%async_computation.9 | async-start | bytes 786432 | tf_op jit(solution)/shard_map/reduce_scatter | solution.py:51
Sparse Core Ops, SparseCore 0:
  124.0 21.0 reduce-scatter.3
  262.2 6.3 reduce-scatter.5
  385.7 6.3 reduce-scatter.7
where the time goes:
time: 404 us; the launch traced here: 403 us
  blocking collectives  208 us (51%)
  waiting for transfers between devices  118 us (29%)
  local copies, waits for them, and re-layouts  28.7 us (7%)
  matrix products  18.9 us (5%)
  between operations  13.3 us (3%)
  starting transfers between devices  13.1 us (3%)
    all_to_all x2, blocking collectives, shards(): lax.all_to_all(outgoing, 'row', split_axis=0, concat_axis=0, tiled=True)  202 us
    all_to_all x1, waiting for transfers between devices, shards(): lax.all_to_all(outgoing, 'row', split_axis=0, concat_axis=0, tiled=True)  78.3 us
    reduce_scatter x3, waiting for transfers between devices, shards(): lax.psum_scatter(partial_value.astype(jnp.bfloat16), 'col', scatter_dimen...  34.2 us
    gather x3, local copies, waits for them, and re-layouts, shards(): flattened[slot_place]  14.8 us
    dot_general x3, matrix products, shards(): jnp.einsum('bkij,bkjr->bir', masked, picked, preferred_element_type=jnp.f...  14.1 us
    gather x3, local copies, waits for them, and re-layouts, shards(): solved[wanted]  9.16 us
    all_to_all x1, starting transfers between devices, shards(): lax.all_to_all(requests.reshape(row_count, capacity), 'row', split_axis=0...  8.34 us
  transfers between devices with their start and end apart: 5, of which 5 were waited for; matrix products, arithmetic and copies ran while one was open for 0% of the time, Pallas kernels for 0%

commit v1 on v0

v1 whole, which is shorter than its diff:
```python
import functools

import jax
import jax.numpy as jnp
from jax import lax
from jax.experimental import pallas as pl
from jax.experimental.pallas import tpu as pltpu
from jax.sharding import PartitionSpec as P

ITERS = 4
MESH = pl.DeviceIdType.MESH
PIECES = ("zxy", "zyx", "xyz", "yxz")
EIGHTHS = (3, 3, 1, 1)
TO_X, TO_Y, TO_UP, TO_DOWN, TO_COL = range(5)


def kernel(
    n_row,
    n_col,
    columns,
    rhs_hbm,
    inv_hbm,
    off_hbm,
    out,
    xg,
    off,
    rhs,
    inv,
    mine,
    outgoing,
    incoming,
    load_sem,
    recv_sem,
    send_sem,
    col_sem,
    part_send,
    part_recv,
    out_send,
    out_recv,
    ready,
):
    row, col = lax.axis_index("row"), lax.axis_index("col")
    block_rows, per_group, size = off.shape[0], off.shape[1], off.shape[2]
    share = block_rows // n_col
    by_blocks = share % 8 == 0
    n_z = n_row // 4
    x, y, z = row % 2, (row // 2) % 2, row // 4
    has_up, has_down = z < n_z - 1, z > 0
    target_row = {
        TO_X: row + 1 - 2 * x,
        TO_Y: row + 2 - 4 * y,
        TO_UP: row + 4,
        TO_DOWN: row - 4,
    }
    back = {TO_X: TO_X, TO_Y: TO_Y, TO_UP: TO_DOWN, TO_DOWN: TO_UP}
    others = [(col + step) % n_col for step in range(1, n_col)]

    loads = []
    first = col * share
    for number, (src, dst) in enumerate(
        (
            (rhs_hbm.at[pl.ds(first, share)], rhs),
            (inv_hbm.at[pl.ds(first, share)], inv),
            (off_hbm, off),
        )
    ):
        copy = pltpu.make_async_copy(src, dst, load_sem.at[number])
        copy.start()
        loads.append(copy)

    def greet(semaphore_of):
        for to in (TO_X, TO_Y):
            pl.semaphore_signal(
                semaphore_of(back[to]), inc=1, device_id=(target_row[to], col), device_id_type=MESH
            )
        for to, there in ((TO_UP, has_up), (TO_DOWN, has_down)):

            @pl.when(there)
            def _():
                pl.semaphore_signal(
                    semaphore_of(back[to]),
                    inc=1,
                    device_id=(target_row[to], col),
                    device_id_type=MESH,
                )

        for step, other in enumerate(others):
            pl.semaphore_signal(
                semaphore_of(TO_COL + step), inc=1, device_id=(row, other), device_id_type=MESH
            )

    barrier = pltpu.get_barrier_semaphore()
    greet(lambda which: barrier)
    pl.semaphore_wait(
        barrier, 2 + len(others) + has_up.astype(jnp.int32) + has_down.astype(jnp.int32)
    )

    def start_of(of_col, of_row):
        return (of_col * n_row + of_row) * share

    def whole_share(of_col, of_row):
        return xg.at[pl.ds(start_of(of_col, of_row), share)]

    def piece_of(piece, src):
        begin, eighths = sum(EIGHTHS[:piece]), EIGHTHS[piece]
        if by_blocks:
            return xg.at[pl.ds(start_of(col, src) + begin * share // 8, eighths * share // 8)]
        rows = size // 8
        return xg.at[pl.ds(start_of(col, src), share), pl.ds(begin * rows, eighths * rows)]

    def eighths_of_share(eighths):
        if by_blocks:
            return xg.at[pl.ds(0, eighths * share // 8)]
        return xg.at[pl.ds(0, eighths * share), pl.ds(0, size // 8)]

    def remote(piece, src, to):
        return pltpu.make_async_remote_copy(
            src_ref=piece_of(piece, src),
            dst_ref=piece_of(piece, src),
            send_sem=send_sem.at[to],
            recv_sem=recv_sem.at[piece, src],
            device_id=(target_row[to], col),
            device_id_type=MESH,
        )

    def send(piece, src, to):
        remote(piece, src, to).start()

    def arrived(piece, src):
        remote(piece, src, TO_X).wait_recv()

    def send_z(piece, src, ways=(TO_UP, TO_DOWN)):
        for to in ways:

            @pl.when(has_up if to == TO_UP else has_down)
            def _():
                send(piece, src, to)

    def share_copy(src, step):
        return pltpu.make_async_remote_copy(
            src_ref=whole_share(col, src),
            dst_ref=whole_share(col, src),
            send_sem=send_sem.at[TO_COL + step],
            recv_sem=col_sem.at[step, src],
            device_id=(row, others[step]),
            device_id_type=MESH,
        )

    def at(plane, flip_y, flip_x):
        there_y = 1 - y if flip_y else y
        there_x = 1 - x if flip_x else x
        return plane * 4 + there_y * 2 + there_x

    FLIPS = ((0, 0), (0, 1), (1, 0), (1, 1))

    def spread_plane(plane):
        arrived(0, at(plane, 0, 1))
        send(0, at(plane, 0, 1), TO_Y)
        arrived(1, at(plane, 1, 0))
        send(1, at(plane, 1, 0), TO_X)
        arrived(0, at(plane, 1, 0))
        arrived(1, at(plane, 0, 1))
        arrived(0, at(plane, 1, 1))
        arrived(1, at(plane, 1, 1))

    def to_columns(plane, own):
        for flip in FLIPS:
            if own and flip == (0, 0):
                continue
            for step in range(n_col - 1):
                share_copy(at(plane, *flip), step).start()

    def gather():
        send(2, row, TO_X)
        send(3, row, TO_Y)
        send(3, row, TO_X)
        send(2, row, TO_Y)
        for piece in range(4):
            send_z(piece, row)
        send(1, row, TO_X)
        send(0, row, TO_Y)
        send(0, row, TO_X)
        send(1, row, TO_Y)
        for step in range(n_col - 1):
            share_copy(row, step).start()
        arrived(2, at(z, 0, 1))
        send(2, at(z, 0, 1), TO_Y)
        send_z(2, at(z, 0, 1))
        arrived(3, at(z, 1, 0))
        send(3, at(z, 1, 0), TO_X)
        send_z(3, at(z, 1, 0))
        for piece, flips in ((2, ((1, 0), (1, 1))), (3, ((0, 1), (1, 1)))):
            for flip in flips:
                arrived(piece, at(z, *flip))
                send_z(piece, at(z, *flip))

        for distance in range(1, n_z + 1):
            for sign, onward in ((-1, TO_UP), (1, TO_DOWN)):
                plane = z + sign * distance
                there = plane >= 0 if sign < 0 else plane < n_z

                if distance < n_z:

                    @pl.when(there)
                    def _():
                        for piece in (0, 1):
                            src = at(plane, 0, 0)
                            arrived(piece, src)
                            send_z(piece, src, (onward,))
                            for to in (TO_X, TO_Y) if piece == 1 else (TO_Y, TO_X):
                                send(piece, src, to)
                        for piece in (2, 3):
                            for flip in FLIPS:
                                arrived(piece, at(plane, *flip))
                                send_z(piece, at(plane, *flip), (onward,))

                if distance == 1:
                    if sign < 0:
                        spread_plane(z)
                        to_columns(z, True)
                    continue
                before = z + sign * (distance - 1)
                was_there = before >= 0 if sign < 0 else before < n_z

                @pl.when(was_there)
                def _():
                    spread_plane(before)
                    to_columns(before, False)

        for step in range(n_col - 1):
            sender = others[n_col - 2 - step]
            for src in range(n_row):
                pltpu.make_async_remote_copy(
                    src_ref=whole_share(sender, src),
                    dst_ref=whole_share(sender, src),
                    send_sem=send_sem.at[TO_COL + step],
                    recv_sem=col_sem.at[step, src],
                    device_id=(row, others[step]),
                    device_id_type=MESH,
                ).wait_recv()

    def sent(to, eighths):
        part = eighths_of_share(eighths)
        pltpu.make_async_copy(part, part, send_sem.at[to]).wait()

    def finish_sends():
        for to in (TO_X, TO_Y):
            sent(to, n_z * 9 + 3)
        for to, there, ahead in ((TO_UP, has_up, z), (TO_DOWN, has_down, n_z - 1 - z)):
            for earlier in range(n_z - 1):

                @pl.when(jnp.logical_and(there, earlier <= ahead))
                def _():
                    sent(to, 14)

        for step in range(n_col - 1):
            sent(TO_COL + step, 8 * n_row)

    def product(i):
        left = jnp.concatenate([off[i, k] for k in range(per_group)], axis=1)
        right = jnp.concatenate(
            [xg[columns[i * per_group + k]] for k in range(per_group)], axis=0
        )
        return jnp.dot(left, right, preferred_element_type=jnp.float32).astype(jnp.bfloat16)

    def part_copy(step):
        return pltpu.make_async_remote_copy(
            src_ref=outgoing.at[step],
            dst_ref=incoming.at[step],
            send_sem=part_send.at[step],
            recv_sem=part_recv.at[step],
            device_id=(row, others[step]),
            device_id_type=MESH,
        )

    own_start = start_of(col, row)

    xg[n_col * n_row * share] = jnp.zeros(xg.shape[1:], xg.dtype)
    loads[0].wait()
    loads[1].wait()

    for j in range(share):
        solved = jnp.dot(inv[j], rhs[j], preferred_element_type=jnp.float32)
        xg[own_start + j] = solved.astype(jnp.bfloat16)
    loads[2].wait()

    def iterate(turn, carry):
        @pl.when(turn > 0)
        def _():
            for to in (TO_X, TO_Y):
                pl.semaphore_wait(ready.at[to], 1)
            for to, there in ((TO_UP, has_up), (TO_DOWN, has_down)):

                @pl.when(there)
                def _():
                    pl.semaphore_wait(ready.at[to], 1)

            for step in range(n_col - 1):
                pl.semaphore_wait(ready.at[TO_COL + step], 1)

        gather()
        finish_sends()
        for step in range(n_col - 1):
            for j in range(share):
                outgoing[step, j] = product(others[step] * share + j)
            part_copy(step).start()
        for j in range(share):
            mine[j] = product(col * share + j).astype(jnp.float32)

        @pl.when(turn < ITERS - 2)
        def _():
            greet(lambda which: ready.at[which])

        for step in range(n_col - 1):
            part_copy(step).wait()
        for j in range(share):
            total = mine[j]
            for step in range(n_col - 1):
                total = total + incoming[step, j].astype(jnp.float32)
            corrected = (rhs[j].astype(jnp.float32) - total).astype(jnp.bfloat16)
            solved = jnp.dot(inv[j], corrected, preferred_element_type=jnp.float32)
            xg[own_start + j] = solved.astype(jnp.bfloat16)
        return carry

    lax.fori_loop(0, ITERS - 1, iterate, 0)

    def out_copy(step):
        part = out.at[pl.ds(col * share, share)]
        return pltpu.make_async_remote_copy(
            src_ref=whole_share(col, row),
            dst_ref=part,
            send_sem=out_send.at[step],
            recv_sem=out_recv.at[step],
            device_id=(row, others[step]),
            device_id_type=MESH,
        )

    for step in range(n_col - 1):
        out_copy(step).start()
    out[pl.ds(col * share, share)] = xg[pl.ds(own_start, share)]
    for step in range(n_col - 1):
        out_copy(step).wait()


def shards(n_row, n_col, right_sides, inverse_diag, off_blocks, owners, local_block, counts):
    block_rows, size, width = right_sides.shape
    per_group = owners.shape[2]
    share = block_rows // n_col
    slot = lax.axis_index("col") + n_col * jnp.arange(per_group, dtype=jnp.int32)
    place = local_block[0]
    found = (place // share) * (n_row * share) + owners[0] * share + place % share
    columns = jnp.where(slot[None, :] < counts[:, None], found, n_row * block_rows).reshape(-1)
    smem = pl.BlockSpec(memory_space=pltpu.SMEM)
    hbm = pl.BlockSpec(memory_space=pl.ANY)
    bf16 = jnp.bfloat16
    dma = pltpu.SemaphoreType.DMA
    return pl.pallas_call(
        functools.partial(kernel, n_row, n_col),
        out_shape=jax.ShapeDtypeStruct(right_sides.shape, bf16),
        in_specs=[smem, hbm, hbm, hbm],
        out_specs=pl.BlockSpec(memory_space=pltpu.VMEM),
        scratch_shapes=[
            pltpu.VMEM((n_row * block_rows + 1, size, width), bf16),
            pltpu.VMEM((block_rows, per_group, size, size), bf16),
            pltpu.VMEM((share, size, width), bf16),
            pltpu.VMEM((share, size, size), bf16),
            pltpu.VMEM((share, size, width), jnp.float32),
            pltpu.VMEM((n_col - 1, share, size, width), bf16),
            pltpu.VMEM((n_col - 1, share, size, width), bf16),
            dma((3,)),
            dma((4, n_row)),
            dma((4 + n_col - 1,)),
            dma((n_col - 1, n_row)),
            dma((n_col - 1,)),
            dma((n_col - 1,)),
            dma((n_col - 1,)),
            dma((n_col - 1,)),
            pltpu.SemaphoreType.REGULAR((4 + n_col - 1,)),
        ],
        compiler_params=pltpu.CompilerParams(
            collective_id=0, has_side_effects=True, vmem_limit_bytes=60 * 1024 * 1024
        ),
    )(
        columns,
        right_sides,
        inverse_diag,
        off_blocks.reshape(off_blocks.shape[1:]),
    )


def solution(mesh):
    in_specs = (
        P("row", None, None),
        P("row", None, None),
        P("col", "row", None, None, None),
        P("col", "row", None),
        P("col", "row", None),
        P("row"),
    )
    body = functools.partial(shards, mesh.shape["row"], mesh.shape["col"])
    return jax.shard_map(
        body, mesh=mesh, in_specs=in_specs, out_specs=P("row", None, None), check_vma=False
    )
```

time: 404 us -> 158 us (0.39)
  blocking collectives: 208 us -> 0 us
  Pallas kernels: 0 us -> 153 us
  waiting for transfers between devices: 118 us -> 0 us
  local copies, waits for them, and re-layouts: 28.7 us -> 3 us
  matrix products: 18.9 us -> 0 us
  between operations: 13.3 us -> 0.02 us
  starting transfers between devices: 13.1 us -> 0 us
    all_to_all x2 -> x0, blocking collectives: 202 us -> none  [shards(): lax.all_to_all(outgoing, 'row', split_axis=0, concat_axis=0, tiled=True)]
    pallas_call x0 -> x1, Pallas kernels: none -> 153 us  [shards(): pl.pallas_call(functools.partial(kernel, n_row, n_col), out_shape=jax.Sha...]
    all_to_all x2 -> x0, waiting for transfers between devices: 84.2 us -> none  [the longest x1 78.3 us: shards(): lax.all_to_all(outgoing, 'row', split_axis=0, concat_axis=0, tiled=True)]
    reduce_scatter x3 -> x0, waiting for transfers between devices: 34.2 us -> none  [shards(): lax.psum_scatter(partial_value.astype(jnp.bfloat16), 'col', scatter_dimen...]
    gather x6 -> x0, local copies, waits for them, and re-layouts: 23.9 us -> none  [the longest x3 14.8 us: shards(): flattened[slot_place]]
    dot_general x7 -> x0, matrix products: 18.9 us -> none  [the longest x3 14.1 us: shards(): jnp.einsum('bkij,bkjr->bir', masked, picked, preferred_element_type=jnp.f...]
    all_to_all x2 -> x0, starting transfers between devices: 13 us -> none  [the longest x1 8.34 us: shards(): lax.all_to_all(requests.reshape(row_count, capacity), 'row', split_axis=0...]
    all_gather x3 -> x0, blocking collectives: 6.54 us -> none  [shards(): lax.all_gather(apply_inverse(inverse_part, corrected), 'col', axis=0, til...]
  transfers between devices with their start and end apart: 5 -> 0, of which waited for: 5 -> 0; matrix products, arithmetic and copies ran while one was open for 0% -> 0% of each run, Pallas kernels for 0% -> 0%
where the time goes in v1:
time: 158 us
  Pallas kernels  153 us (97%)
  local copies, waits for them, and re-layouts  3 us (2%)
  other arithmetic  1.95 us (1%)
    pallas_call x1, Pallas kernels, shards(): pl.pallas_call(functools.partial(kernel, n_row, n_col), out_shape=jax.Sha...  153 us

profile of v1, /device:TPU:0, one launch (start us, length us, event | category | flops | bytes accessed | tf_op | source)
XLA Modules:
  0.0 158.2 jit_solution(1207311690046652339)
XLA Ops:
  0.0 0.7 broadcast_compare_fusion
  0.7 0.1 lt.26
  0.8 0.7 broadcast_multiply_fusion
  1.5 0.1 copy.10
  1.6 0.1 mul.26
  1.7 0.8 copy.9
  2.5 0.1 squeeze.4
  2.6 0.5 fusion.1.columns
  3.1 153.2 %shard_map.64 = bf16[16,128,128]{2,1,0:T(8,128)(2,1)} custom-call(s32[96]{0:T(128)} %fusion.1.columns, bf16[16,128,128]{2,1,0:T(8,128)(2,1)} %rhs_hbm.1, bf16[16,128,128]{2,1,0:T(8,128)(2,1)} %inv_hbm.1, bf16[16,6,128,128]{3,2,1,0:T(8,128)(2,1)} %bitcast.1), custom_call_target="tpu_custom_call" | custom-call | tf_op jit(solution)/shard_map/pallas_call | solution.py:357
  156.3 1.9 %copy.12 = bf16[16,128,128]{2,1,0:T(8,128)(2,1)} copy(bf16[16,128,128]{2,1,0:T(8,128)(2,1)} %shard_map.64) | data formatting | bytes 1048576
  (1 shorter events, 0.0 us)

commit v2 on v1

--- a/solution.py
+++ b/solution.py
@@ -1,4 +1,5 @@
 import functools
+import heapq
 
 import jax
 import jax.numpy as jnp
@@ -9,9 +10,94 @@
 
 ITERS = 4
 MESH = pl.DeviceIdType.MESH
-PIECES = ("zxy", "zyx", "xyz", "yxz")
-EIGHTHS = (3, 3, 1, 1)
 TO_X, TO_Y, TO_UP, TO_DOWN, TO_COL = range(5)
+FOUR = (3, 3, 1, 1)
+EIGHT = (1,) * 8
+EDGE = ("zxy", "zyx", "zxy", "xzy", "yxz", "yzx", "zyx", "xzy")
+INNER = ("zyx", "zxy", "zyx", "yzx", "xzy", "zxy", "zyx", "yxz")
+ORDERS = ("zxy", "zyx", "xyz", "yxz", "xzy", "yzx")
+DEPTH_WEIGHT, DISTANCE_WEIGHT = 0.73, 0.08
+PLANE_WEIGHT = dict(zip(ORDERS, (0.62, -0.3, -0.43, -0.82, 0.14, 0.07)))
+LINE_WEIGHT = dict(zip(ORDERS, (-1.84, -0.38, 0.41, -1.4, -1.52, -2.03)))
+PIECE_TIME, LATENCY, AHEAD = 0.703, 1.6, 1.5
+
+
+def targets(order, n_z, z, src_z, flip_y, flip_x):
+    moved = {"x": flip_x, "y": flip_y, "z": src_z != z}
+    found = []
+    for place, axis in enumerate(order):
+        if any(moved[later] for later in order[place + 1 :]):
+            continue
+        if axis == "z":
+            if src_z <= z < n_z - 1:
+                found.append(TO_UP)
+            if src_z >= z > 0:
+                found.append(TO_DOWN)
+        elif not moved[axis]:
+            found.append(TO_X if axis == "x" else TO_Y)
+    return found
+
+
+def beyond(z, src_z, flip_y, flip_x, to):
+    return {
+        TO_X: (z, src_z, flip_y, 1 - flip_x),
+        TO_Y: (z, src_z, 1 - flip_y, flip_x),
+        TO_UP: (z + 1, src_z, flip_y, flip_x),
+        TO_DOWN: (z - 1, src_z, flip_y, flip_x),
+    }[to]
+
+
+@functools.lru_cache(None)
+def depth(order, n_z, *where):
+    ways = targets(order, n_z, *where)
+    return max((1 + depth(order, n_z, *beyond(*where, to)) for to in ways), default=0)
+
+
+def planned(n_z):
+    orders = [EDGE if z in (0, n_z - 1) else INNER for z in range(n_z)]
+    events, queued, busy = [], {}, {}
+    log = [[] for _ in range(n_z)]
+    count = 0
+    for z in range(n_z):
+        for piece in range(len(EIGHT)):
+            events.append((0.0, count, None, piece, (z, z, 0, 0)))
+            count += 1
+    heapq.heapify(events)
+    while events:
+        now, touched = events[0][0], set()
+        while events and events[0][0] <= now + 1e-9:
+            _, _, link, piece, where = heapq.heappop(events)
+            if link is not None:
+                busy[link] = False
+                touched.add(link)
+                continue
+            z, src_z, flip_y, flip_x = where
+            if where != (z, z, 0, 0):
+                log[z].append((now, 0, count, (piece, src_z, flip_y, flip_x)))
+            order = orders[src_z][piece]
+            for to in targets(order, n_z, *where):
+                weight = PLANE_WEIGHT if to in (TO_X, TO_Y) else LINE_WEIGHT
+                rank = (
+                    weight[order]
+                    + DISTANCE_WEIGHT * abs(src_z - z)
+                    - DEPTH_WEIGHT * depth(order, n_z, *beyond(*where, to))
+                )
+                heapq.heappush(queued.setdefault((z, to), []), (rank, now, count, piece, where))
+                touched.add((z, to))
+                count += 1
+        for link in sorted(touched):
+            if busy.get(link) or not queued.get(link):
+                continue
+            _, known, _, piece, where = heapq.heappop(queued[link])
+            z, to = link
+            busy[link] = True
+            log[z].append((max(known, now - AHEAD), 1, count, (piece, *where[1:], to)))
+            heapq.heappush(events, (now + PIECE_TIME, count + 1, link, None, None))
+            heapq.heappush(
+                events, (now + PIECE_TIME + LATENCY, count + 2, None, piece, beyond(*where, to))
+            )
+            count += 3
+    return [[entry[3] for entry in sorted(one)] for one in log]
 
 
 def kernel(
@@ -43,6 +129,8 @@
     block_rows, per_group, size = off.shape[0], off.shape[1], off.shape[2]
     share = block_rows // n_col
     by_blocks = share % 8 == 0
+    short = n_row // 4 <= 4
+    eighths_of = EIGHT if short else FOUR
     n_z = n_row // 4
     x, y, z = row % 2, (row // 2) % 2, row // 4
     has_up, has_down = z < n_z - 1, z > 0
@@ -96,13 +184,15 @@
     )
 
     def start_of(of_col, of_row):
-        return (of_col * n_row + of_row) * share
+        return of_row * block_rows + of_col * share
 
     def whole_share(of_col, of_row):
         return xg.at[pl.ds(start_of(of_col, of_row), share)]
 
     def piece_of(piece, src):
-        begin, eighths = sum(EIGHTHS[:piece]), EIGHTHS[piece]
+        return part_of(src, sum(eighths_of[:piece]), eighths_of[piece])
+
+    def part_of(src, begin, eighths):
         if by_blocks:
             return xg.at[pl.ds(start_of(col, src) + begin * share // 8, eighths * share // 8)]
         rows = size // 8
@@ -136,10 +226,10 @@
             def _():
                 send(piece, src, to)
 
-    def share_copy(src, step):
+    def share_copy(src, step, begin=0, eighths=8):
         return pltpu.make_async_remote_copy(
-            src_ref=whole_share(col, src),
-            dst_ref=whole_share(col, src),
+            src_ref=part_of(src, begin, eighths),
+            dst_ref=part_of(src, begin, eighths),
             send_sem=send_sem.at[TO_COL + step],
             recv_sem=col_sem.at[step, src],
             device_id=(row, others[step]),
@@ -227,6 +317,28 @@
                     spread_plane(before)
                     to_columns(before, False)
 
+    def gather_by_plan(my_z, plan):
+        have = {}
+        sent_to = dict.fromkeys((TO_X, TO_Y, TO_UP, TO_DOWN), 0)
+        for step in range(n_col - 1):
+            share_copy(row, step).start()
+        for piece, src_z, flip_y, flip_x, *to in plan:
+            src = at(src_z, flip_y, flip_x)
+            if to:
+                send(piece, src, to[0])
+                sent_to[to[0]] += 1
+                continue
+            arrived(piece, src)
+            half = (src_z, flip_y, flip_x, piece // 4)
+            have[half] = have.get(half, 0) + 1
+            if have[half] == 4:
+                for step in range(n_col - 1):
+                    share_copy(src, step, piece // 4 * 4, 4).start()
+        for to, number in sent_to.items():
+            if number:
+                sent(to, number)
+
+    def finish_columns():
         for step in range(n_col - 1):
             sender = others[n_col - 2 - step]
             for src in range(n_row):
@@ -238,6 +350,7 @@
                     device_id=(row, others[step]),
                     device_id_type=MESH,
                 ).wait_recv()
+            sent(TO_COL + step, 8 * n_row)
 
     def sent(to, eighths):
         part = eighths_of_share(eighths)
@@ -253,8 +366,6 @@
                 def _():
                     sent(to, 14)
 
-        for step in range(n_col - 1):
-            sent(TO_COL + step, 8 * n_row)
 
     def product(i):
         left = jnp.concatenate([off[i, k] for k in range(per_group)], axis=1)
@@ -298,8 +409,13 @@
             for step in range(n_col - 1):
                 pl.semaphore_wait(ready.at[TO_COL + step], 1)
 
-        gather()
-        finish_sends()
+        if short:
+            for my_z, plan in enumerate(planned(n_z)):
+                pl.when(z == my_z)(functools.partial(gather_by_plan, my_z, plan))
+        else:
+            gather()
+            finish_sends()
+        finish_columns()
         for step in range(n_col - 1):
             for j in range(share):
                 outgoing[step, j] = product(others[step] * share + j)
@@ -347,8 +463,7 @@
     per_group = owners.shape[2]
     share = block_rows // n_col
     slot = lax.axis_index("col") + n_col * jnp.arange(per_group, dtype=jnp.int32)
-    place = local_block[0]
-    found = (place // share) * (n_row * share) + owners[0] * share + place % share
+    found = owners[0] * block_rows + local_block[0]
     columns = jnp.where(slot[None, :] < counts[:, None], found, n_row * block_rows).reshape(-1)
     smem = pl.BlockSpec(memory_space=pltpu.SMEM)
     hbm = pl.BlockSpec(memory_space=pl.ANY)
@@ -368,7 +483,7 @@
             pltpu.VMEM((n_col - 1, share, size, width), bf16),
             pltpu.VMEM((n_col - 1, share, size, width), bf16),
             dma((3,)),
-            dma((4, n_row)),
+            dma((8, n_row)),
             dma((4 + n_col - 1,)),
             dma((n_col - 1, n_row)),
             dma((n_col - 1,)),

time: 158 us -> 120 us (0.76)
  Pallas kernels: 153 us -> 116 us
    pallas_call x1, Pallas kernels: 153 us -> 116 us  [shards(): pl.pallas_call(functools.partial(kernel, n_row, n_col), out_shape=jax.Sha...]
where the time goes in v2:
time: 120 us
  Pallas kernels  116 us (97%)
  local copies, waits for them, and re-layouts  2.15 us (2%)
  other arithmetic  1.96 us (2%)
    pallas_call x1, Pallas kernels, shards(): pl.pallas_call(functools.partial(kernel, n_row, n_col), out_shape=jax.Sha...  116 us

profile of v2, /device:TPU:0, one launch (start us, length us, event | category | flops | bytes accessed | tf_op | source)
XLA Modules:
  0.0 120.2 jit_solution(4634992595346927549)
XLA Ops:
  0.0 0.7 broadcast_compare_fusion
  0.7 0.1 lt.20
  0.8 0.7 multiply_add_fusion
  1.5 0.1 copy.8
  1.6 0.1 add.20
  1.7 0.5 broadcast_select_fusion.columns
  2.2 116.0 %shard_map.64 = bf16[16,128,128]{2,1,0:T(8,128)(2,1)} custom-call(s32[96]{0:T(128)} %broadcast_select_fusion.columns, bf16[16,128,128]{2,1,0:T(8,128)(2,1)} %rhs_hbm.1, bf16[16,128,128]{2,1,0:T(8,128)(2,1)} %inv_hbm.1, bf16[16,6,128,128]{3,2,1,0:T(8,128)(2,1)} %bitcast.1), custom_call_target="tpu_custom_call" | custom-call | tf_op jit(solution)/shard_map/pallas_call | solution.py:472
  118.3 1.9 %copy.10 = bf16[16,128,128]{2,1,0:T(8,128)(2,1)} copy(bf16[16,128,128]{2,1,0:T(8,128)(2,1)} %shard_map.64) | data formatting | bytes 1048576
  (1 shorter events, 0.0 us)

commit v3 on v2

--- a/solution.py
+++ b/solution.py
@@ -19,7 +19,7 @@
 DEPTH_WEIGHT, DISTANCE_WEIGHT = 0.73, 0.08
 PLANE_WEIGHT = dict(zip(ORDERS, (0.62, -0.3, -0.43, -0.82, 0.14, 0.07)))
 LINE_WEIGHT = dict(zip(ORDERS, (-1.84, -0.38, 0.41, -1.4, -1.52, -2.03)))
-PIECE_TIME, LATENCY, AHEAD = 0.703, 1.6, 1.5
+PIECE_TIME, LATENCY, AHEAD = 0.72, 2.4, 1.2
 
 
 def targets(order, n_z, z, src_z, flip_y, flip_x):
@@ -370,7 +370,7 @@
     def product(i):
         left = jnp.concatenate([off[i, k] for k in range(per_group)], axis=1)
         right = jnp.concatenate(
-            [xg[columns[i * per_group + k]] for k in range(per_group)], axis=0
+            [xg[columns[k, i]] for k in range(per_group)], axis=0
         )
         return jnp.dot(left, right, preferred_element_type=jnp.float32).astype(jnp.bfloat16)
 
@@ -462,9 +462,11 @@
     block_rows, size, width = right_sides.shape
     per_group = owners.shape[2]
     share = block_rows // n_col
-    slot = lax.axis_index("col") + n_col * jnp.arange(per_group, dtype=jnp.int32)
-    found = owners[0] * block_rows + local_block[0]
-    columns = jnp.where(slot[None, :] < counts[:, None], found, n_row * block_rows).reshape(-1)
+    slot = lax.axis_index("col") + n_col * lax.broadcasted_iota(
+        jnp.int32, (per_group, block_rows), 0
+    )
+    found = owners[0].T * block_rows + local_block[0].T
+    columns = jnp.where(slot < counts[None, :], found, n_row * block_rows)
     smem = pl.BlockSpec(memory_space=pltpu.SMEM)
     hbm = pl.BlockSpec(memory_space=pl.ANY)
     bf16 = jnp.bfloat16

time: 120 us -> 113 us (0.942)
  Pallas kernels: 116 us -> 110 us
    pallas_call x1, Pallas kernels: 116 us -> 110 us  [shards(): pl.pallas_call(functools.partial(kernel, n_row, n_col), out_shape=jax.Sha...]
where the time goes in v3:
time: 113 us
  Pallas kernels  110 us (97%)
  local copies, waits for them, and re-layouts  1.89 us (2%)
  other arithmetic  1.37 us (1%)
    pallas_call x1, Pallas kernels, shards(): pl.pallas_call(functools.partial(kernel, n_row, n_col), out_shape=jax.Sha...  110 us

profile of v3, /device:TPU:0, one launch (start us, length us, event | category | flops | bytes accessed | tf_op | source)
XLA Modules:
  0.0 113.2 jit_solution(13912985522960683747)
XLA Ops:
  0.0 1.4 %bitcast_select_fusion.columns = s32[6,16]{1,0:T(8,128)} fusion(s32[1,16,6]{1,0,2:T(1,128)} %param.10, s32[1,16,6]{1,0,2:T(1,128)} %param.9, s32[16]{0:T(128)} %param.11, s32[6]{0:T(128)S(1)} %multiply_add_fusion), kind=kLoop, calls=%fused_computation | loop fusion | flops 384 | bytes 1240 | tf_op jit(solution)/shard_map/jit(_where)/select_n | solution.py:469
  1.4 110.0 %shard_map.64 = bf16[16,128,128]{2,1,0:T(8,128)(2,1)} custom-call(s32[6,16]{1,0:T(8,128)} %bitcast_select_fusion.columns, bf16[16,128,128]{2,1,0:T(8,128)(2,1)} %rhs_hbm.1, bf16[16,128,128]{2,1,0:T(8,128)(2,1)} %inv_hbm.1, bf16[16,6,128,128]{3,2,1,0:T(8,128)(2,1)} %bitcast.5), custom_call_target="tpu_custom_call" | custom-call | tf_op jit(solution)/shard_map/pallas_call | solution.py:474
  111.3 1.9 %copy.16 = bf16[16,128,128]{2,1,0:T(8,128)(2,1)} copy(bf16[16,128,128]{2,1,0:T(8,128)(2,1)} %shard_map.64) | data formatting | bytes 1048576
  (1 shorter events, 0.0 us)
